TPU v7x, 128 devices: a whole 4x4x4 slice. The times are simulated.
128 devices in a mesh: sp: 8 (over x, y_lo), ep: 16 (over z, y_hi, core).
Axes of the slice: x: 4, y: 4 (y_hi: 2, y_lo: 2; y = y_hi * 2 + y_lo), z: 4, core: 2. Of those that a mesh axis runs over, the one named last changes fastest.
Arguments:
- residual: bfloat16 [16384, 4096], P(('sp', 'ep')), may hold values from -40 to 40
- queries: bfloat16 [16384, 4096], P(('sp', 'ep')), may hold values from -6 to 6
- key_rows: bfloat16 [16384, 1024], P(('sp', 'ep')), may hold values from -6 to 6
- value_rows: bfloat16 [16384, 1024], P(('sp', 'ep')), may hold values from -6 to 6
- visible: int32 [128, 9], replicated, may hold values from 0 to 1, as said below
- out_proj: bfloat16 [4096, 4096], P(('sp', 'ep')), may hold values from -0.09375 to 0.09375
- norm_gain: float32 [4096], replicated, may hold values from 0.5 to 1.5
- expert_ids: int32 [16384, 2], P(('sp', 'ep')), may hold values from 0 to 7, all different within a row; in each aligned block of 128 rows (0 to 127, 128 to 255, ...) at most 40 rows name the same one
- route_weight: float32 [16384, 2], P(('sp', 'ep')), may hold values from 0.2 to 1
- expert_gate: bfloat16 [2, 7168, 4096], P(None, 'ep'), may hold values from -0.09375 to 0.09375
- expert_up: bfloat16 [2, 7168, 4096], P(None, 'ep'), may hold values from -0.09375 to 0.09375
- expert_down: bfloat16 [2, 7168, 4096], P(None, 'ep'), may hold values from -0.0625 to 0.0625
Outputs:
- layer_out: bfloat16 [16384, 4096], P(('sp', 'ep'))
Inputs may be any that keep to these rules, and one draw needn't show every extreme that they name: The sequence is packed with documents that are runs of whole blocks of 128 tokens, the first of them 9 blocks or longer; visible[q, d] is 1 exactly when block q - d exists and lies in the document of block q, so visible[q, 0] = 1. `expert_ids`: each token names two different experts. Among the 128 tokens of one block no expert is named by more than 40 tokens.
All inputs are finite; a program needn't handle non-finite values.
Results may differ from a plain program's by a relative error of at most 0.0065.
Values may be sent and summed in bfloat16 or wider, within the bound.
No kernel may reach another device: no remote copies, remote signals or barrier semaphores. Data moves between devices by JAX's collectives and lax.ppermute only.
A program may use at most 128 MiB of HBM per device.

v0:
```python
import math

import jax
import jax.numpy as jnp
from jax import lax
from jax.experimental import pallas as pl
from jax.experimental.pallas import tpu as pltpu
from jax.sharding import Mesh
from jax.sharding import PartitionSpec as P


HEAD = 128
CAP = 40
SIZES = (4, 2, 4, 2, 2)
AXES = ("x", "yl", "z", "h", "c")
EP = ("z", "h", "c")


def flat(coords):
    place = 0
    for size, coord in zip(SIZES, coords):
        place = place * size + coord
    return place


def sent(value, rule):
    pairs = []
    for source in range(math.prod(SIZES)):
        rest, coords = source, []
        for size in reversed(SIZES):
            coords.append(rest % size)
            rest //= size
        cx, cyl, cz, ch, cc = reversed(coords)
        x, y, z, core = rule(cx, 2 * ch + cyl, cz, cc)
        pairs.append((source, flat((x % 4, y % 2, z % 4, y % 4 // 2, core))))
    return lax.ppermute(value, AXES, pairs)


def moved(value, x=0, y=0, z=0):
    return sent(value, lambda cx, cy, cz, cc: (cx + x, cy + y, cz + z, cc))


def crossed(value):
    return sent(value, lambda cx, cy, cz, cc: (cx, cy, cz, 1 - cc))


def mate(place, pairing):
    return place + (1 if (place + pairing) % 2 == 0 else -1)


def to_mate(value, along_x, along_z, switch):
    def rule(cx, cy, cz, cc):
        goal = 1 - cc if switch else cc
        return (mate(cx, goal) if along_x else cx, cy, mate(cz, goal) if along_z else cz, goal)

    return sent(value, rule)


def from_mate(value, along_x, along_z, switch):
    def rule(cx, cy, cz, cc):
        goal = 1 - cc if switch else cc
        return (mate(cx, cc) if along_x else cx, cy, mate(cz, cc) if along_z else cz, goal)

    return sent(value, rule)


def later(value, blocks, switch):
    count = math.prod(SIZES)
    return lax.ppermute(
        value, AXES, [(s, (s ^ switch) + blocks) for s in range(count - blocks)]
    )


def half_of(value, which):
    width = value.shape[-1] // 2
    return lax.dynamic_slice_in_dim(value, which * width, width, value.ndim - 1)


def by_core(first, own, other, axis):
    return jnp.where(
        first,
        jnp.concatenate([own, other], axis=axis),
        jnp.concatenate([other, own], axis=axis),
    )


def attend_kernel(core_ref, seen_ref, query_ref, *refs):
    key_refs, value_refs, (out_ref, key_table, value_table) = refs[:10], refs[10:20], refs[20:]
    core = core_ref[0]
    for place in range(10):
        slot = place - place % 2 + (1 - core if place % 2 else core)
        key_table[slot] = key_refs[place][...]
        value_table[slot] = value_refs[place][...]
    factor = math.log2(math.e) / math.sqrt(HEAD)
    tokens = 128
    row = lax.broadcasted_iota(jnp.int32, (tokens, tokens), 0)
    col = lax.broadcasted_iota(jnp.int32, (tokens, tokens), 1)
    causal = jnp.where(col <= row, 0.0, -1e30)

    @pl.loop(0, 2)
    def _(block):
        here = pl.ds(pl.multiple_of(block * tokens, tokens), tokens)
        key_window = key_table[pl.ds(block, 9)].reshape(-1, HEAD)
        value_window = value_table[pl.ds(block, 9)].reshape(-1, HEAD)
        hidden = [
            jnp.full((tokens, tokens), jnp.where(seen_ref[block, 8 - place] > 0, 0.0, -1e30))
            for place in range(8)
        ]
        bias = jnp.concatenate(hidden + [causal], axis=1)
        query = jnp.concatenate(
            [query_ref[here, head * HEAD : (head + 1) * HEAD] for head in range(4)], axis=0
        )
        scores = lax.dot_general(
            query, key_window, (((1,), (1,)), ((), ())), preferred_element_type=jnp.float32
        )
        weights, totals = [], []
        for head in range(4):
            score = scores[head * tokens : (head + 1) * tokens] + bias
            peak = jnp.max(score, axis=1, keepdims=True)
            weight = jnp.exp2((score - peak) * factor)
            totals.append(jnp.sum(weight, axis=1, keepdims=True))
            weights.append(weight.astype(jnp.bfloat16))
        mixed = jnp.dot(
            jnp.concatenate(weights, axis=0), value_window, preferred_element_type=jnp.float32
        )
        for head in range(4):
            result = mixed[head * tokens : (head + 1) * tokens] / totals[head]
            lanes = slice(head // 2 * HEAD, head // 2 * HEAD + HEAD)
            out_ref[0, head % 2, here, lanes] = result.astype(jnp.bfloat16)


def attend(core, seen, query, windows):
    key_specs = [pl.BlockSpec((128, HEAD), lambda j: (0, j)) for _ in windows]
    value_specs = [pl.BlockSpec((128, HEAD), lambda j: (0, 4 + j)) for _ in windows]
    return pl.pallas_call(
        attend_kernel,
        grid=(4,),
        in_specs=[
            pl.BlockSpec(memory_space=pltpu.SMEM),
            pl.BlockSpec(memory_space=pltpu.SMEM),
            pl.BlockSpec((256, 4 * HEAD), lambda j: (0, j)),
            *key_specs,
            *value_specs,
        ],
        out_specs=pl.BlockSpec((1, 2, 256, 256), lambda j: (j // 2, 0, 0, j % 2)),
        out_shape=jax.ShapeDtypeStruct((2, 2, 256, 512), jnp.bfloat16),
        scratch_shapes=[
            pltpu.VMEM((10, 128, HEAD), jnp.bfloat16),
            pltpu.VMEM((10, 128, HEAD), jnp.bfloat16),
        ],
        name="attend",
        cost_estimate=pl.CostEstimate(
            flops=6_000_000_000, transcendentals=5_000_000, bytes_accessed=6_000_000
        ),
    )(core.reshape(1), seen, query, *windows, *windows)


def in_order(pieces, own_index):
    count = len(pieces)
    table = jnp.zeros((count, *pieces[0].shape), pieces[0].dtype)
    for step, piece in enumerate(pieces):
        table = lax.dynamic_update_index_in_dim(table, piece, (own_index - step) % count, 0)
    return table


def by_height(pieces, place_y):
    x_half, z_half, rows, columns = pieces[0][2].shape
    table = jnp.zeros((x_half, 2, z_half, 2, rows, columns), pieces[0][2].dtype)
    for step, column, piece in pieces:
        source = (place_y - step) % 4
        piece = piece.reshape(x_half, 1, z_half, 1, rows, -1)
        table = lax.dynamic_update_slice(table, piece, (0, source % 2, 0, source // 2, 0, column))
    return table


def project_kernel(core_ref, *refs):
    same, other, (rows_own, rows_other) = refs[:8], refs[8:16], refs[16:18]
    left = jnp.concatenate([ref[0] for ref in same], axis=0)
    right = jnp.concatenate([ref[0] for ref in other], axis=0)
    product = jnp.dot(left, rows_own[0], preferred_element_type=jnp.float32)
    product += jnp.dot(right, rows_other[0], preferred_element_type=jnp.float32)
    product = product.astype(jnp.bfloat16)
    for place, out_ref in enumerate(refs[18:]):
        out_ref[...] = product[place * 128 : (place + 1) * 128]


def project(core, same, other, rows):
    columns = 512
    same = [heads.reshape(2, 128, 512) for heads in same for _ in range(2)]
    other = [heads.reshape(2, 128, 512) for heads in other for _ in range(2)]
    here = pl.BlockSpec((1, 128, 512), lambda n, core: (core[0], 0, 0))
    there = pl.BlockSpec((1, 128, 512), lambda n, core: (1 - core[0], 0, 0))
    out = pl.BlockSpec((128, columns), lambda n, core: (0, n))
    shape = jax.ShapeDtypeStruct((128, rows.shape[2]), jnp.bfloat16)
    return pl.pallas_call(
        project_kernel,
        grid_spec=pltpu.PrefetchScalarGridSpec(
            num_scalar_prefetch=1,
            grid=(4,),
            in_specs=[
                *[here, there] * 8,
                pl.BlockSpec((1, 512, columns), lambda n, core: (core[0], 0, n)),
                pl.BlockSpec((1, 512, columns), lambda n, core: (1 - core[0], 0, n)),
            ],
            out_specs=[out] * 8,
        ),
        out_shape=[shape] * 8,
        name="project",
        cost_estimate=pl.CostEstimate(
            flops=4_300_000_000, transcendentals=0, bytes_accessed=10_000_000
        ),
    )(core.reshape(1), *same, *other, rows, rows)


def expert_kernel(*refs):
    slot_refs, (gate_ref, up_ref, down_ref, own_ref, other_ref) = refs[:4], refs[4:9]
    gate_sum, up_sum, act = refs[9:]
    step = pl.program_id(0)
    contract = (((1,), (1,)), ((), ()))

    @pl.when(step == 0)
    def _():
        gate_sum[...] = jnp.zeros_like(gate_sum)
        up_sum[...] = jnp.zeros_like(up_sum)

    @pl.when(step < 2)
    def _():
        slots = jnp.concatenate([ref[...] for ref in slot_refs], axis=0)
        gate = lax.dot_general(slots, gate_ref[0], contract, preferred_element_type=jnp.float32)
        up = lax.dot_general(slots, up_ref[0], contract, preferred_element_type=jnp.float32)
        gate_sum[...] += gate
        up_sum[...] += up

        @pl.when(step == 1)
        def _():
            value = gate_sum[...]
            act[...] = (value / (1.0 + jnp.exp(-value)) * up_sum[...]).astype(jnp.bfloat16)

    @pl.when(step >= 2)
    def _():
        result = jnp.dot(act[...], down_ref[0], preferred_element_type=jnp.float32)
        result = result.astype(jnp.bfloat16)
        half = result.shape[0] // 2
        own_ref[...] = result[:half]
        other_ref[...] = result[half:]


def expert(which, pieces, gate, up, down):
    slots, width = pieces[0].shape
    hidden = gate.shape[1]
    chunk = width // 2
    rows = len(pieces) * slots
    early = lambda step: jnp.minimum(step, 1)
    late = lambda step: jnp.maximum(step - 2, 0)
    out = pl.BlockSpec((rows // 2, chunk), lambda step: (0, late(step)))
    shape = jax.ShapeDtypeStruct((rows // 2, width), jnp.bfloat16)
    return pl.pallas_call(
        expert_kernel,
        grid=(4,),
        in_specs=[
            *[pl.BlockSpec((slots, chunk), lambda step: (0, early(step))) for _ in pieces],
            pl.BlockSpec((1, hidden, chunk), lambda step: (which, 0, early(step))),
            pl.BlockSpec((1, hidden, chunk), lambda step: (which, 0, early(step))),
            pl.BlockSpec((1, hidden, chunk), lambda step: (which, 0, late(step))),
        ],
        out_specs=[out, out],
        out_shape=[shape, shape],
        scratch_shapes=[
            pltpu.VMEM((rows, hidden), jnp.float32),
            pltpu.VMEM((rows, hidden), jnp.float32),
            pltpu.VMEM((rows, hidden), jnp.bfloat16),
        ],
        name="expert",
        cost_estimate=pl.CostEstimate(
            flops=7_000_000_000, transcendentals=300_000, bytes_accessed=22_000_000
        ),
    )(*pieces, gate, up, down)


def total(*terms):
    return sum(term.astype(jnp.float32) for term in terms).astype(jnp.bfloat16)


def gather_slots(own):
    flip = moved(own, y=2)
    far = moved(own, z=2)
    flip_far = moved(far, y=2)
    both = jnp.concatenate([own, flip], axis=0)
    ring1, ring3 = moved(both, z=1), moved(both, z=3)
    early = jnp.concatenate([both, far, flip_far], axis=0)
    early_got = crossed(early)
    late = jnp.concatenate([ring1, ring3], axis=0)
    late_got = crossed(late)
    return [early, late, early_got, late_got]


def return_sums(own_part, other_part):
    swapped = crossed(other_part)

    def owed(place, count=1):
        rows = slice(place * CAP, (place + count) * CAP)
        return total(own_part[rows], swapped[rows])

    here, flip, far, flip_far, ring1, ring3 = lax.optimization_barrier(
        (owed(0), owed(1), owed(2), owed(3), owed(4, 2), owed(6, 2))
    )
    flip_far = moved(flip_far, y=2)
    ring1, ring3 = moved(ring1, z=3), moved(ring3, z=1)
    across = moved(total(flip, ring1[CAP:], ring3[CAP:]), y=2)
    twice = moved(total(far, flip_far), z=2)
    return sum(t.astype(jnp.float32) for t in (here, ring1[:CAP], ring3[:CAP], across, twice))


def local(
    residual,
    queries,
    key_rows,
    value_rows,
    visible,
    out_proj,
    norm_gain,
    expert_ids,
    route_weight,
    expert_gate,
    expert_up,
    expert_down,
):
    core = lax.axis_index("c")
    first = core == 0
    tokens = residual.shape[0]
    place_x, place_z = lax.axis_index("x"), lax.axis_index("z")
    place_y = 2 * lax.axis_index("h") + lax.axis_index("yl")

    kv_own = jnp.concatenate([half_of(key_rows, core), half_of(value_rows, core)], axis=1)
    kv_give = jnp.concatenate([half_of(key_rows, 1 - core), half_of(value_rows, 1 - core)], axis=1)
    kv_got = crossed(kv_give)
    query_got = crossed(half_of(queries, 1 - core))
    query_two = by_core(first, half_of(queries, core), query_got, 0)
    windows = []
    for blocks in (8, 6, 4, 2):
        windows += [later(kv_own, blocks, 0), later(kv_give, blocks, 1)]
    windows += [kv_own, kv_got]

    columns = out_proj.shape[1] // 2
    rows_got = moved(out_proj, z=2)
    rows = in_order([out_proj, rows_got], place_z // 2)
    rows_got = crossed(half_of(rows, 1 - core))
    rows = by_core(first, half_of(rows, core), rows_got, 1)
    rows_got = moved(rows, x=2)
    rows = in_order([rows, rows_got], place_x // 2)
    rows_up, rows_down = moved(rows, y=1), moved(rows, y=3)
    half = columns // 2
    far_low, far_high = moved(rows_up[..., :half], y=1), moved(rows_down[..., half:], y=3)
    pieces = [(0, 0, rows), (1, 0, rows_up), (3, 0, rows_down), (2, 0, far_low), (2, half, far_high)]
    rows = by_height(pieces, place_y).reshape(2, -1, columns)

    chip_block = lax.axis_index(AXES) - core
    seen = lax.dynamic_slice_in_dim(visible, chip_block, 2, 0)
    attended = attend(core, seen, query_two, windows)
    attended = attended.reshape(4, 2 * tokens, -1)

    ways = ((1, 1), (1, 0), (0, 1), (0, 0))
    same, other = [], []
    for along_x, along_z in ways:
        wanted = (place_x % 2 ^ along_x) * 2 + (place_z % 2 ^ along_z)
        piece = lax.dynamic_index_in_dim(attended, wanted, 0, keepdims=False)
        remote = along_x or along_z
        same.append(to_mate(piece, along_x, along_z, False) if remote else piece)
        other.append(to_mate(piece, along_x, along_z, True) if remote else crossed(piece))
    products = project(core, same, other, rows)
    straight, switched = [], []
    for place, (along_x, along_z) in enumerate(ways):
        here, there = products[2 * place : 2 * place + 2]
        if along_x or along_z:
            here = from_mate(here, along_x, along_z, False)
            there = from_mate(there, along_x, along_z, True)
        else:
            there = crossed(there)
        straight.append(here.astype(jnp.float32))
        switched.append(there.astype(jnp.float32))
    projected = by_core(first, sum(straight), sum(switched), 1)

    hidden_sum = residual.astype(jnp.float32) + projected
    mean_square = jnp.mean(hidden_sum * hidden_sum, axis=-1, keepdims=True)
    normed = (hidden_sum * lax.rsqrt(mean_square + 1e-05) * norm_gain).astype(jnp.bfloat16)

    mixes, slots = [], []
    for which in range(expert_gate.shape[0]):
        choose = expert_ids == which
        member = jnp.any(choose, axis=1)
        token_weight = jnp.sum(jnp.where(choose, route_weight, 0.0), axis=1)
        ranked = jnp.cumsum(member.astype(jnp.int32)) - member.astype(jnp.int32)
        slot_hit = (ranked[None, :] == jnp.arange(CAP, dtype=jnp.int32)[:, None]) & member[None, :]
        slots.append(slot_hit.astype(jnp.bfloat16))
        mixes.append(jnp.where(slot_hit, token_weight[None, :], 0.0))
    outgoing = jnp.dot(
        jnp.concatenate(slots, axis=0), normed, preferred_element_type=jnp.float32
    ).astype(jnp.bfloat16)

    returned = []
    for which in range(expert_gate.shape[0]):
        pieces = gather_slots(outgoing[which * CAP : (which + 1) * CAP])
        parts = expert(which, pieces, expert_gate, expert_up, expert_down)
        returned.append(return_sums(*parts))
    expert_mix = jnp.dot(
        jnp.concatenate(mixes, axis=0).T,
        jnp.concatenate(returned, axis=0),
        precision=lax.Precision.HIGHEST,
    )
    return (hidden_sum + expert_mix).astype(jnp.bfloat16)


def solution(mesh):
    finer = Mesh(mesh.devices.reshape(SIZES), AXES)
    in_specs = (
        P(AXES, None),
        P(AXES, None),
        P(AXES, None),
        P(AXES, None),
        P(),
        P(AXES, None),
        P(),
        P(AXES, None),
        P(AXES, None),
        P(None, EP, None),
        P(None, EP, None),
        P(None, EP, None),
    )
    return jax.shard_map(
        local, mesh=finer, in_specs=in_specs, out_specs=P(AXES, None), check_vma=False
    )
```

profile of v0, /device:TPU:0, one launch (start us, length us, event | category | flops | bytes accessed | tf_op | source)
XLA Modules:
  0.0 312.1 jit_solution(6635072345983936589)
XLA Ops:
  1.3 6.7 %collective-permute-start.1 = (bf16[128,1024]{1,0:T(8,128)(2,1)S(1)}, bf16[128,1024]{1,0:T(8,128)(2,1)}, u32[]{:S(2)}, u32[]{:S(2)}) collective-permute-start(bf16[128,1024]{1,0:T(8,128)(2,1)S(1)} %pad_maximum_fusion.4.refs_8_.refs_18_), channel_id=1, source_target_pairs={{0,8},{1,9},{2,10},{3,11},{4,12},{5,13},{6,14},{7,15},{8,16},{9,17... | collective-permute-start | bytes 786440 | tf_op jit(solution)/shard_map/ppermute | solution.py:69
  8.0 6.3 %collective-permute-start.3 = (bf16[128,1024]{1,0:T(8,128)(2,1)S(1)}, bf16[128,1024]{1,0:T(8,128)(2,1)}, u32[]{:S(2)}, u32[]{:S(2)}) collective-permute-start(bf16[128,1024]{1,0:T(8,128)(2,1)S(1)} %pad_maximum_fusion.4.refs_8_.refs_18_), channel_id=1, source_target_pairs={{0,6},{1,7},{2,8},{3,9},{4,10},{5,11},{6,12},{7,13},{8,14},{9,15},... | collective-permute-start | bytes 786440 | tf_op jit(solution)/shard_map/ppermute | solution.py:69
  16.5 5.7 %collective-permute-start.2 = (bf16[128,1024]{1,0:T(8,128)(2,1)}, bf16[128,1024]{1,0:T(8,128)(2,1)}, u32[]{:S(2)}, u32[]{:S(2)}) collective-permute-start(bf16[128,1024]{1,0:T(8,128)(2,1)} %pad_maximum_fusion.5), channel_id=1, source_target_pairs={{0,9},{1,8},{2,11},{3,10},{4,13},{5,12},{6,15},{7,14},{8,17},{9,16... | collective-permute-start | bytes 786440 | tf_op jit(solution)/shard_map/ppermute | solution.py:69
  27.7 11.1 %collective-permute-start.19 = (bf16[2,64,2048]{2,1,0:T(8,128)(2,1)}, bf16[2,64,2048]{2,1,0:T(8,128)(2,1)S(1)}, u32[]{:S(2)}, u32[]{:S(2)}) collective-permute-start(bf16[2,64,2048]{2,1,0:T(8,128)(2,1)} %maximum_select_fusion.3), channel_id=1, source_target_pairs={{0,64},{1,65},{2,66},{3,67},{4,68},{5,69},{6,70},{7,71},{8,72},{9,... | collective-permute-start | bytes 1572872 | tf_op jit(solution)/shard_map/ppermute | solution.py:36
  48.1 5.0 %collective-permute-start.7 = (bf16[128,1024]{1,0:T(8,128)(2,1)S(1)}, bf16[128,1024]{1,0:T(8,128)(2,1)S(1)}, u32[]{:S(2)}, u32[]{:S(2)}) collective-permute-start(bf16[128,1024]{1,0:T(8,128)(2,1)S(1)} %pad_maximum_fusion.4.refs_8_.refs_18_), channel_id=1, source_target_pairs={{0,2},{1,3},{2,4},{3,5},{4,6},{5,7},{6,8},{7,9},{8,10},{9,11},{10,... | collective-permute-start | bytes 786440 | tf_op jit(solution)/shard_map/ppermute | solution.py:69
  59.7 12.8 %collective-permute-done.6.refs_5_.refs_15_ = bf16[128,1024]{1,0:T(8,128)(2,1)} collective-permute-done((bf16[128,1024]{1,0:T(8,128)(2,1)}, bf16[128,1024]{1,0:T(8,128)(2,1)}, u32[]{:S(2)}, u32[]{:S(2)}) %collective-permute-start.6) | collective-permute-done | bytes 262176 | tf_op jit(solution)/shard_map/ppermute | solution.py:69
  74.6 15.8 %attend.1 = bf16[2,2,256,512]{3,2,1,0:T(8,128)(2,1)} custom-call(s32[1]{0:T(128)} %bitcast.core_ref, s32[2,9]{1,0:T(2,128)} %copy.27.seen_ref, bf16[256,2048]{1,0:T(8,128)(2,1)} %maximum_select_fusion.1.query_ref, bf16[128,1024]{1,0:T(8,128)(2,1)} %collective-permute-done.1.refs_0_.refs_10_, bf16[128,1024]{1,0:T(8,128)(2,1)} %collective-permute-done.2.refs_1_.refs_11_, ...), custom_call_target="tpu_custom_call" | custom-call | flops 6000000000 | bytes 6000000 | tf_op jit(solution)/shard_map/attend/pallas_call | solution.py:135
  91.7 6.1 %collective-permute-start.14 = (bf16[256,512]{1,0:T(8,128)(2,1)S(1)}, bf16[256,512]{1,0:T(8,128)(2,1)S(1)}, u32[]{:S(2)}, u32[]{:S(2)}) collective-permute-start(bf16[256,512]{1,0:T(8,128)(2,1)S(1)} %get-tuple-element.71), channel_id=1, source_target_pairs={{0,97},{1,32},{2,99},{3,34},{4,101},{5,36},{6,103},{7,38},{8,105},... | collective-permute-start | bytes 786440 | tf_op jit(solution)/shard_map/ppermute | solution.py:36
  97.8 4.2 %collective-permute-start.11 = (bf16[256,512]{1,0:T(8,128)(2,1)S(1)}, bf16[256,512]{1,0:T(8,128)(2,1)S(1)}, u32[]{:S(2)}, u32[]{:S(2)}) collective-permute-start(bf16[256,512]{1,0:T(8,128)(2,1)S(1)} %get-tuple-element.71), channel_id=1, source_target_pairs={{0,32},{1,97},{2,34},{3,99},{4,36},{5,101},{6,38},{7,103},{8,40},{... | collective-permute-start | bytes 786440 | tf_op jit(solution)/shard_map/ppermute | solution.py:36
  112.8 8.7 %collective-permute-done.22 = bf16[2,2,64,1024]{3,2,1,0:T(8,128)(2,1)S(1)} collective-permute-done((bf16[2,2,64,1024]{3,2,1,0:T(8,128)(2,1)S(1)}, bf16[2,2,64,1024]{3,2,1,0:T(8,128)(2,1)S(1)}, u32[]{:S(2)}, u32[]{:S(2)}) %collective-permute-start.22) | collective-permute-done | bytes 524320 | tf_op jit(solution)/shard_map/ppermute | solution.py:36
  123.4 4.8 %collective-permute-done.13 = bf16[256,512]{1,0:T(8,128)(2,1)S(1)} collective-permute-done((bf16[256,512]{1,0:T(8,128)(2,1)S(1)}, bf16[256,512]{1,0:T(8,128)(2,1)S(1)}, u32[]{:S(2)}, u32[]{:S(2)}) %collective-permute-start.13) | collective-permute-done | bytes 262176 | tf_op jit(solution)/shard_map/ppermute | solution.py:36
  128.9 8.3 %project.1 = (bf16[128,2048]{1,0:T(8,128)(2,1)}, bf16[128,2048]{1,0:T(8,128)(2,1)}, bf16[128,2048]{1,0:T(8,128)(2,1)}, bf16[128,2048]{1,0:T(8,128)(2,1)}, bf16[1...) custom-call(s32[1]{0:T(128)} %bitcast.core_ref, ...), custom_call_target="tpu_custom_call" | custom-call | flops 4300000256 | bytes 10000000 | tf_op jit(solution)/shard_map/project/pallas_call | solution.py:195
  142.6 6.9 %collective-permute-done.27 = bf16[128,2048]{1,0:T(8,128)(2,1)S(1)} collective-permute-done((bf16[128,2048]{1,0:T(8,128)(2,1)}, bf16[128,2048]{1,0:T(8,128)(2,1)S(1)}, u32[]{:S(2)}, u32[]{:S(2)}) %collective-permute-start.27) | collective-permute-done | bytes 524320 | tf_op jit(solution)/shard_map/ppermute | solution.py:36
  153.4 7.4 %collective-permute-done.24 = bf16[128,2048]{1,0:T(8,128)(2,1)S(1)} collective-permute-done((bf16[128,2048]{1,0:T(8,128)(2,1)}, bf16[128,2048]{1,0:T(8,128)(2,1)S(1)}, u32[]{:S(2)}, u32[]{:S(2)}) %collective-permute-start.24) | collective-permute-done | bytes 524320 | tf_op jit(solution)/shard_map/ppermute | solution.py:36
  161.2 5.1 %collective-permute-done.26 = bf16[128,2048]{1,0:T(8,128)(2,1)S(1)} collective-permute-done((bf16[128,2048]{1,0:T(8,128)(2,1)}, bf16[128,2048]{1,0:T(8,128)(2,1)S(1)}, u32[]{:S(2)}, u32[]{:S(2)}) %collective-permute-start.26) | collective-permute-done | bytes 524320 | tf_op jit(solution)/shard_map/ppermute | solution.py:36
  175.3 5.0 %collective-permute-done.31 = bf16[40,4096]{1,0:T(8,128)(2,1)S(1)} collective-permute-done((bf16[40,4096]{1,0:T(8,128)(2,1)S(1)}, bf16[40,4096]{1,0:T(8,128)(2,1)S(1)}, u32[]{:S(2)}, u32[]{:S(2)}) %collective-permute-start.31) | collective-permute-done | bytes 327712 | tf_op jit(solution)/shard_map/ppermute | solution.py:36
  193.6 6.8 %collective-permute-done.34 = bf16[80,4096]{1,0:T(8,128)(2,1)S(1)} collective-permute-done((bf16[80,4096]{1,0:T(8,128)(2,1)S(1)}, bf16[80,4096]{1,0:T(8,128)(2,1)S(1)}, u32[]{:S(2)}, u32[]{:S(2)}) %collective-permute-start.34) | collective-permute-done | bytes 655392 | tf_op jit(solution)/shard_map/ppermute | solution.py:36
  202.1 12.3 %collective-permute-done.47 = bf16[80,4096]{1,0:T(8,128)(2,1)S(1)} collective-permute-done((bf16[80,4096]{1,0:T(8,128)(2,1)S(1)}, bf16[80,4096]{1,0:T(8,128)(2,1)S(1)}, u32[]{:S(2)}, u32[]{:S(2)}) %collective-permute-start.47) | collective-permute-done | bytes 655392 | tf_op jit(solution)/shard_map/ppermute | solution.py:36
  217.3 14.5 %expert.2 = (bf16[320,4096]{1,0:T(8,128)(2,1)}, bf16[320,4096]{1,0:T(8,128)(2,1)}) custom-call(bf16[160,4096]{1,0:T(8,128)(2,1)} %copy-done.2, bf16[160,4096]{1,0:T(8,128)(2,1)} %copy-done.8, bf16[160,4096]{1,0:T(8,128)(2,1)} %copy-done.11, bf16[160,4096]{1,0:T(8,128)(2,1)} %collective-permute-done.37.refs_3_, bf16[2,448,4096]{2,1,0:T(8,128)(2,1)} %refs_4_.3, ...), custom_call_target="tpu_custom_call" | custom-call | flops 7000000000 | bytes 22000000 | tf_op jit(solution)/shard_map/expert/pallas_call | solution.py:257
  232.5 14.6 %expert.3 = (bf16[320,4096]{1,0:T(8,128)(2,1)}, bf16[320,4096]{1,0:T(8,128)(2,1)}) custom-call(bf16[160,4096]{1,0:T(8,128)(2,1)} %copy-done.3, bf16[160,4096]{1,0:T(8,128)(2,1)} %constant_dynamic-update-slice_fusion.2.refs_1_, bf16[160,4096]{1,0:T(8,128)(2,1)} %collective-permute-done.49.refs_2_, bf16[160,4096]{1,0:T(8,128)(2,1)} %collective-permute-done.50.refs_3_, ...), custom_call_target="tpu_custom_call" | custom-call | flops 7000000000 | bytes 22000000 | tf_op jit(solution)/shard_map/expert/pallas_call | solution.py:257
  259.5 4.9 %collective-permute-done.42 = bf16[40,4096]{1,0:T(8,128)(2,1)S(1)} collective-permute-done((bf16[40,4096]{1,0:T(8,128)(2,1)S(1)}, bf16[40,4096]{1,0:T(8,128)(2,1)S(1)}, u32[]{:S(2)}, u32[]{:S(2)}) %collective-permute-start.42) | collective-permute-done | bytes 327712 | tf_op jit(solution)/shard_map/ppermute | solution.py:36
  267.7 6.9 %collective-permute-done.55 = bf16[40,4096]{1,0:T(8,128)(2,1)S(1)} collective-permute-done((bf16[40,4096]{1,0:T(8,128)(2,1)S(1)}, bf16[40,4096]{1,0:T(8,128)(2,1)S(1)}, u32[]{:S(2)}, u32[]{:S(2)}) %collective-permute-start.55) | collective-permute-done | bytes 327712 | tf_op jit(solution)/shard_map/ppermute | solution.py:36
  283.1 15.0 %collective-permute-done.53 = bf16[80,4096]{1,0:T(8,128)(2,1)S(1)} collective-permute-done((bf16[80,4096]{1,0:T(8,128)(2,1)S(1)}, bf16[80,4096]{1,0:T(8,128)(2,1)S(1)}, u32[]{:S(2)}, u32[]{:S(2)}) %collective-permute-start.53) | collective-permute-done | bytes 655392 | tf_op jit(solution)/shard_map/ppermute | solution.py:36
  301.7 7.0 %collective-permute-done.54 = bf16[40,4096]{1,0:T(8,128)(2,1)S(1)} collective-permute-done((bf16[40,4096]{1,0:T(8,128)(2,1)S(1)}, bf16[40,4096]{1,0:T(8,128)(2,1)S(1)}, u32[]{:S(2)}, u32[]{:S(2)}) %collective-permute-start.54) | collective-permute-done | bytes 327712 | tf_op jit(solution)/shard_map/ppermute | solution.py:36
  (223 shorter events, 109.1 us)
Async XLA Ops:
  1.3 41.1 %collective-permute-start.1 = (bf16[128,1024]{1,0:T(8,128)(2,1)S(1)}, bf16[128,1024]{1,0:T(8,128)(2,1)}, u32[]{:S(2)}, u32[]{:S(2)}) collective-permute-start(bf16[128,1024]{1,0:T(8,128)(2,1)S(1)} %pad_maximum_fusion.4.refs_8_.refs_18_), channel_id=1, source_target_pairs={{0,8},{1,9},{2,10},{3,11},{4,12},{5,13},{6,14},{7,15},{8,16},{9,17... | collective-permute-start | bytes 786440 | tf_op jit(solution)/shard_map/ppermute | solution.py:69
  8.0 40.1 %collective-permute-start.3 = (bf16[128,1024]{1,0:T(8,128)(2,1)S(1)}, bf16[128,1024]{1,0:T(8,128)(2,1)}, u32[]{:S(2)}, u32[]{:S(2)}) collective-permute-start(bf16[128,1024]{1,0:T(8,128)(2,1)S(1)} %pad_maximum_fusion.4.refs_8_.refs_18_), channel_id=1, source_target_pairs={{0,6},{1,7},{2,8},{3,9},{4,10},{5,11},{6,12},{7,13},{8,14},{9,15},... | collective-permute-start | bytes 786440 | tf_op jit(solution)/shard_map/ppermute | solution.py:69
  15.7 23.9 %collective-permute-start = (bf16[128,2048]{1,0:T(8,128)(2,1)}, bf16[128,2048]{1,0:T(8,128)(2,1)S(1)}, u32[]{:S(2)}, u32[]{:S(2)}) collective-permute-start(bf16[128,2048]{1,0:T(8,128)(2,1)} %get-tuple-element.74), channel_id=1, source_target_pairs={{0,1},{1,0},{2,3},{3,2},{4,5},{5,4},{6,7},{7,6},{8,9},{9,8},{10,11... | collective-permute-start | bytes 1572872 | tf_op jit(solution)/shard_map/ppermute | solution.py:36
  16.5 29.4 %collective-permute-start.2 = (bf16[128,1024]{1,0:T(8,128)(2,1)}, bf16[128,1024]{1,0:T(8,128)(2,1)}, u32[]{:S(2)}, u32[]{:S(2)}) collective-permute-start(bf16[128,1024]{1,0:T(8,128)(2,1)} %pad_maximum_fusion.5), channel_id=1, source_target_pairs={{0,9},{1,8},{2,11},{3,10},{4,13},{5,12},{6,15},{7,14},{8,17},{9,16... | collective-permute-start | bytes 786440 | tf_op jit(solution)/shard_map/ppermute | solution.py:69
  27.7 29.7 %collective-permute-start.19 = (bf16[2,64,2048]{2,1,0:T(8,128)(2,1)}, bf16[2,64,2048]{2,1,0:T(8,128)(2,1)S(1)}, u32[]{:S(2)}, u32[]{:S(2)}) collective-permute-start(bf16[2,64,2048]{2,1,0:T(8,128)(2,1)} %maximum_select_fusion.3), channel_id=1, source_target_pairs={{0,64},{1,65},{2,66},{3,67},{4,68},{5,69},{6,70},{7,71},{8,72},{9,... | collective-permute-start | bytes 1572872 | tf_op jit(solution)/shard_map/ppermute | solution.py:36
  45.9 26.6 %collective-permute-start.6 = (bf16[128,1024]{1,0:T(8,128)(2,1)}, bf16[128,1024]{1,0:T(8,128)(2,1)}, u32[]{:S(2)}, u32[]{:S(2)}) collective-permute-start(bf16[128,1024]{1,0:T(8,128)(2,1)} %pad_maximum_fusion.5), channel_id=1, source_target_pairs={{0,5},{1,4},{2,7},{3,6},{4,9},{5,8},{6,11},{7,10},{8,13},{9,12},{1... | collective-permute-start | bytes 786440 | tf_op jit(solution)/shard_map/ppermute | solution.py:69
  48.1 24.4 %collective-permute-start.7 = (bf16[128,1024]{1,0:T(8,128)(2,1)S(1)}, bf16[128,1024]{1,0:T(8,128)(2,1)S(1)}, u32[]{:S(2)}, u32[]{:S(2)}) collective-permute-start(bf16[128,1024]{1,0:T(8,128)(2,1)S(1)} %pad_maximum_fusion.4.refs_8_.refs_18_), channel_id=1, source_target_pairs={{0,2},{1,3},{2,4},{3,5},{4,6},{5,7},{6,8},{7,9},{8,10},{9,11},{10,... | collective-permute-start | bytes 786440 | tf_op jit(solution)/shard_map/ppermute | solution.py:69
  58.2 47.5 %collective-permute-start.20 = (bf16[2,2,64,2048]{3,2,1,0:T(8,128)(2,1)S(1)}, bf16[2,2,64,2048]{3,2,1,0:T(8,128)(2,1)S(1)}, u32[]{:S(2)}, u32[]{:S(2)}) collective-permute-start(bf16[2,2,64,2048]{3,2,1,0:T(8,128)(2,1)S(1)} %bitcast_dynamic-update-slice_fusion.5), channel_id=1, source_target_pairs={{0,16},{1,17},{2,18},{3,19},{4,20},{5,21},{6,22},{7,23},{8,24},{9,... | collective-permute-start | bytes 3145736 | tf_op jit(solution)/shard_map/ppermute | solution.py:36
  72.5 33.3 %collective-permute-start.21 = (bf16[2,2,64,2048]{3,2,1,0:T(8,128)(2,1)S(1)}, bf16[2,2,64,2048]{3,2,1,0:T(8,128)(2,1)S(1)}, u32[]{:S(2)}, u32[]{:S(2)}) collective-permute-start(bf16[2,2,64,2048]{3,2,1,0:T(8,128)(2,1)S(1)} %bitcast_dynamic-update-slice_fusion.5), channel_id=1, source_target_pairs={{0,18},{1,19},{2,16},{3,17},{4,22},{5,23},{6,20},{7,21},{8,26},{9,... | collective-permute-start | bytes 3145736 | tf_op jit(solution)/shard_map/ppermute | solution.py:36
  91.7 19.6 %collective-permute-start.14 = (bf16[256,512]{1,0:T(8,128)(2,1)S(1)}, bf16[256,512]{1,0:T(8,128)(2,1)S(1)}, u32[]{:S(2)}, u32[]{:S(2)}) collective-permute-start(bf16[256,512]{1,0:T(8,128)(2,1)S(1)} %get-tuple-element.71), channel_id=1, source_target_pairs={{0,97},{1,32},{2,99},{3,34},{4,101},{5,36},{6,103},{7,38},{8,105},... | collective-permute-start | bytes 786440 | tf_op jit(solution)/shard_map/ppermute | solution.py:36
  97.8 25.5 %collective-permute-start.11 = (bf16[256,512]{1,0:T(8,128)(2,1)S(1)}, bf16[256,512]{1,0:T(8,128)(2,1)S(1)}, u32[]{:S(2)}, u32[]{:S(2)}) collective-permute-start(bf16[256,512]{1,0:T(8,128)(2,1)S(1)} %get-tuple-element.71), channel_id=1, source_target_pairs={{0,32},{1,97},{2,34},{3,99},{4,36},{5,101},{6,38},{7,103},{8,40},{... | collective-permute-start | bytes 786440 | tf_op jit(solution)/shard_map/ppermute | solution.py:36
  140.4 20.4 %collective-permute-start.24 = (bf16[128,2048]{1,0:T(8,128)(2,1)}, bf16[128,2048]{1,0:T(8,128)(2,1)S(1)}, u32[]{:S(2)}, u32[]{:S(2)}) collective-permute-start(bf16[128,2048]{1,0:T(8,128)(2,1)} %get-tuple-element.29), channel_id=1, source_target_pairs={{0,36},{1,109},{2,38},{3,111},{4,32},{5,105},{6,34},{7,107},{8,44}... | collective-permute-start | bytes 1572872 | tf_op jit(solution)/shard_map/ppermute | solution.py:36
  180.3 20.0 %collective-permute-start.34 = (bf16[80,4096]{1,0:T(8,128)(2,1)S(1)}, bf16[80,4096]{1,0:T(8,128)(2,1)S(1)}, u32[]{:S(2)}, u32[]{:S(2)}) collective-permute-start(bf16[80,4096]{1,0:T(8,128)(2,1)S(1)} %pad_maximum_fusion.2), channel_id=1, source_target_pairs={{0,4},{1,5},{2,6},{3,7},{4,8},{5,9},{6,10},{7,11},{8,12},{9,13},{1... | collective-permute-start | bytes 1966088 | tf_op jit(solution)/shard_map/ppermute | solution.py:36
  180.9 19.5 %collective-permute-start.35 = (bf16[80,4096]{1,0:T(8,128)(2,1)S(1)}, bf16[80,4096]{1,0:T(8,128)(2,1)S(1)}, u32[]{:S(2)}, u32[]{:S(2)}) collective-permute-start(bf16[80,4096]{1,0:T(8,128)(2,1)S(1)} %pad_maximum_fusion.2), channel_id=1, source_target_pairs={{0,12},{1,13},{2,14},{3,15},{4,0},{5,1},{6,2},{7,3},{8,4},{9,5},{1... | collective-permute-start | bytes 1966088 | tf_op jit(solution)/shard_map/ppermute | solution.py:36
  187.4 27.0 %collective-permute-start.47 = (bf16[80,4096]{1,0:T(8,128)(2,1)S(1)}, bf16[80,4096]{1,0:T(8,128)(2,1)S(1)}, u32[]{:S(2)}, u32[]{:S(2)}) collective-permute-start(bf16[80,4096]{1,0:T(8,128)(2,1)S(1)} %pad_maximum_fusion.3), channel_id=1, source_target_pairs={{0,4},{1,5},{2,6},{3,7},{4,8},{5,9},{6,10},{7,11},{8,12},{9,13},{1... | collective-permute-start | bytes 1966088 | tf_op jit(solution)/shard_map/ppermute | solution.py:36
  187.5 27.8 %collective-permute-start.48 = (bf16[80,4096]{1,0:T(8,128)(2,1)S(1)}, bf16[80,4096]{1,0:T(8,128)(2,1)S(1)}, u32[]{:S(2)}, u32[]{:S(2)}) collective-permute-start(bf16[80,4096]{1,0:T(8,128)(2,1)S(1)} %pad_maximum_fusion.3), channel_id=1, source_target_pairs={{0,12},{1,13},{2,14},{3,15},{4,0},{5,1},{6,2},{7,3},{8,4},{9,5},{1... | collective-permute-start | bytes 1966088 | tf_op jit(solution)/shard_map/ppermute | solution.py:36
  202.0 30.6 %collective-permute-start.49 = (bf16[160,4096]{1,0:T(8,128)(2,1)S(1)}, bf16[160,4096]{1,0:T(8,128)(2,1)}, u32[]{:S(2)}, u32[]{:S(2)}) collective-permute-start(bf16[160,4096]{1,0:T(8,128)(2,1)S(1)} %pad_maximum_fusion.1.refs_0_), channel_id=1, source_target_pairs={{0,1},{1,0},{2,3},{3,2},{4,5},{5,4},{6,7},{7,6},{8,9},{9,8},{10,11... | collective-permute-start | bytes 3932168 | tf_op jit(solution)/shard_map/ppermute | solution.py:36
  251.4 23.8 %collective-permute-start.39 = (bf16[80,4096]{1,0:T(8,128)(2,1)S(1)}, bf16[80,4096]{1,0:T(8,128)(2,1)S(1)}, u32[]{:S(2)}, u32[]{:S(2)}) collective-permute-start(bf16[80,4096]{1,0:T(8,128)(2,1)S(1)} %get-tuple-element.40), channel_id=1, source_target_pairs={{0,12},{1,13},{2,14},{3,15},{4,0},{5,1},{6,2},{7,3},{8,4},{9,5},{1... | collective-permute-start | bytes 1966088 | tf_op jit(solution)/shard_map/ppermute | solution.py:36
  252.1 26.2 %collective-permute-start.40 = (bf16[80,4096]{1,0:T(8,128)(2,1)S(1)}, bf16[80,4096]{1,0:T(8,128)(2,1)S(1)}, u32[]{:S(2)}, u32[]{:S(2)}) collective-permute-start(bf16[80,4096]{1,0:T(8,128)(2,1)S(1)} %get-tuple-element.41), channel_id=1, source_target_pairs={{0,4},{1,5},{2,6},{3,7},{4,8},{5,9},{6,10},{7,11},{8,12},{9,13},{1... | collective-permute-start | bytes 1966088 | tf_op jit(solution)/shard_map/ppermute | solution.py:36
  257.4 25.7 %collective-permute-start.52 = (bf16[80,4096]{1,0:T(8,128)(2,1)S(1)}, bf16[80,4096]{1,0:T(8,128)(2,1)S(1)}, u32[]{:S(2)}, u32[]{:S(2)}) collective-permute-start(bf16[80,4096]{1,0:T(8,128)(2,1)S(1)} %get-tuple-element.48), channel_id=1, source_target_pairs={{0,12},{1,13},{2,14},{3,15},{4,0},{5,1},{6,2},{7,3},{8,4},{9,5},{1... | collective-permute-start | bytes 1966088 | tf_op jit(solution)/shard_map/ppermute | solution.py:36
  259.3 38.8 %collective-permute-start.53 = (bf16[80,4096]{1,0:T(8,128)(2,1)S(1)}, bf16[80,4096]{1,0:T(8,128)(2,1)S(1)}, u32[]{:S(2)}, u32[]{:S(2)}) collective-permute-start(bf16[80,4096]{1,0:T(8,128)(2,1)S(1)} %get-tuple-element.49), channel_id=1, source_target_pairs={{0,4},{1,5},{2,6},{3,7},{4,8},{5,9},{6,10},{7,11},{8,12},{9,13},{1... | collective-permute-start | bytes 1966088 | tf_op jit(solution)/shard_map/ppermute | solution.py:36
  274.5 27.0 %collective-permute-start.43 = (bf16[40,4096]{1,0:T(8,128)(2,1)S(1)}, bf16[40,4096]{1,0:T(8,128)(2,1)S(1)}, u32[]{:S(2)}, u32[]{:S(2)}) collective-permute-start(bf16[40,4096]{1,0:T(8,128)(2,1)S(1)} %add_convert_fusion.10), channel_id=1, source_target_pairs={{0,8},{1,9},{2,10},{3,11},{4,12},{5,13},{6,14},{7,15},{8,0},{9,1},... | collective-permute-start | bytes 983048 | tf_op jit(solution)/shard_map/ppermute | solution.py:36
  275.2 26.6 %collective-permute-start.56 = (bf16[40,4096]{1,0:T(8,128)(2,1)S(1)}, bf16[40,4096]{1,0:T(8,128)(2,1)S(1)}, u32[]{:S(2)}, u32[]{:S(2)}) collective-permute-start(bf16[40,4096]{1,0:T(8,128)(2,1)S(1)} %add_convert_fusion.4), channel_id=1, source_target_pairs={{0,8},{1,9},{2,10},{3,11},{4,12},{5,13},{6,14},{7,15},{8,0},{9,1},... | collective-permute-start | bytes 983048 | tf_op jit(solution)/shard_map/ppermute | solution.py:36
  278.4 23.1 %collective-permute-start.41 = (bf16[40,4096]{1,0:T(8,128)(2,1)S(1)}, bf16[40,4096]{1,0:T(8,128)(2,1)S(1)}, u32[]{:S(2)}, u32[]{:S(2)}) collective-permute-start(bf16[40,4096]{1,0:T(8,128)(2,1)S(1)} %add_convert_fusion.11), channel_id=1, source_target_pairs={{0,2},{1,3},{2,0},{3,1},{4,6},{5,7},{6,4},{7,5},{8,10},{9,11},{10,... | collective-permute-start | bytes 983048 | tf_op jit(solution)/shard_map/ppermute | solution.py:36
  (66 other events, 838.9 us)
where the time goes:
time: 313 us; the launch traced here: 312 us
  waiting for transfers between devices  120 us (38%)
  starting transfers between devices  105 us (34%)
  Pallas kernels  53.1 us (17%)
  local copies, waits for them, and re-layouts  18.4 us (6%)
  other arithmetic  10.6 us (3%)
  matrix products  3.77 us (1%)
    ppermute x49, waiting for transfers between devices, sent(): return lax.ppermute(value, AXES, pairs)  107 us
    ppermute x49, starting transfers between devices, sent(): return lax.ppermute(value, AXES, pairs)  70.6 us
    ppermute x8, starting transfers between devices, later(): lax.ppermute(value, AXES, [(s, (s ^ switch) + blocks) for s in range(coun...  34.9 us
    pallas_call x2, Pallas kernels, expert(): pl.pallas_call(expert_kernel, grid=(4,), in_specs=[*[pl.BlockSpec((slots,...  29 us
    pallas_call x1, Pallas kernels, attend(): pl.pallas_call(attend_kernel, grid=(4,), in_specs=[pl.BlockSpec(memory_sp...  15.8 us
    ppermute x8, waiting for transfers between devices, later(): lax.ppermute(value, AXES, [(s, (s ^ switch) + blocks) for s in range(coun...  12.8 us
    pallas_call x1, Pallas kernels, project(): pl.pallas_call(project_kernel, grid_spec=pltpu.PrefetchScalarGridSpec(num...  8.25 us
  transfers between devices with their start and end apart: 57, of which 22 were waited for; matrix products, arithmetic and copies ran while one was open for 7% of the time, Pallas kernels for 14%

commit v1 on v0

--- a/solution.py
+++ b/solution.py
@@ -96,12 +96,12 @@
     row = lax.broadcasted_iota(jnp.int32, (tokens, tokens), 0)
     col = lax.broadcasted_iota(jnp.int32, (tokens, tokens), 1)
     causal = jnp.where(col <= row, 0.0, -1e30)
-
-    @pl.loop(0, 2)
-    def _(block):
-        here = pl.ds(pl.multiple_of(block * tokens, tokens), tokens)
-        key_window = key_table[pl.ds(block, 9)].reshape(-1, HEAD)
-        value_window = value_table[pl.ds(block, 9)].reshape(-1, HEAD)
+    keys = key_table[...].reshape(-1, HEAD)
+    values = value_table[...].reshape(-1, HEAD)
+    for block in range(2):
+        here = slice(block * tokens, (block + 1) * tokens)
+        key_window = keys[block * tokens : (block + 9) * tokens]
+        value_window = values[block * tokens : (block + 9) * tokens]
         hidden = [
             jnp.full((tokens, tokens), jnp.where(seen_ref[block, 8 - place] > 0, 0.0, -1e30))
             for place in range(8)
@@ -238,11 +238,16 @@
 
     @pl.when(step >= 2)
     def _():
-        result = jnp.dot(act[...], down_ref[0], preferred_element_type=jnp.float32)
-        result = result.astype(jnp.bfloat16)
-        half = result.shape[0] // 2
-        own_ref[...] = result[:half]
-        other_ref[...] = result[half:]
+        part, half = 512, own_ref.shape[0]
+
+        @pl.loop(0, own_ref.shape[1] // part)
+        def _(place):
+            lanes = pl.ds(pl.multiple_of(place * part, part), part)
+            result = jnp.dot(
+                act[...], down_ref[0, :, lanes], preferred_element_type=jnp.float32
+            ).astype(jnp.bfloat16)
+            own_ref[:, lanes] = result[:half]
+            other_ref[:, lanes] = result[half:]
 
 
 def expert(which, pieces, gate, up, down):

time: 313 us -> 312 us (level)
  no operation moved by 1% of the time
where the time goes in v1:
time: 312 us; the launch traced here: 311 us
  waiting for transfers between devices  120 us (38%)
  starting transfers between devices  106 us (34%)
  Pallas kernels  52.1 us (17%)
  local copies, waits for them, and re-layouts  18.4 us (6%)
  other arithmetic  10.6 us (3%)
  matrix products  3.76 us (1%)
    ppermute x49, waiting for transfers between devices, sent(): return lax.ppermute(value, AXES, pairs)  107 us
    ppermute x49, starting transfers between devices, sent(): return lax.ppermute(value, AXES, pairs)  70.8 us
    ppermute x8, starting transfers between devices, later(): lax.ppermute(value, AXES, [(s, (s ^ switch) + blocks) for s in range(coun...  34.9 us
    pallas_call x2, Pallas kernels, expert(): pl.pallas_call(expert_kernel, grid=(4,), in_specs=[*[pl.BlockSpec((slots,...  31.1 us
    ppermute x8, waiting for transfers between devices, later(): lax.ppermute(value, AXES, [(s, (s ^ switch) + blocks) for s in range(coun...  12.8 us
    pallas_call x1, Pallas kernels, attend(): pl.pallas_call(attend_kernel, grid=(4,), in_specs=[pl.BlockSpec(memory_sp...  12.8 us
    pallas_call x1, Pallas kernels, project(): pl.pallas_call(project_kernel, grid_spec=pltpu.PrefetchScalarGridSpec(num...  8.24 us
  transfers between devices with their start and end apart: 57, of which 22 were waited for; matrix products, arithmetic and copies ran while one was open for 7% of the time, Pallas kernels for 14%

profile of v1, /device:TPU:0, one launch (start us, length us, event | category | flops | bytes accessed | tf_op | source)
XLA Modules:
  0.0 311.2 jit_solution(15764535648075958175)
XLA Ops:
  1.3 6.7 %collective-permute-start.1 = (bf16[128,1024]{1,0:T(8,128)(2,1)S(1)}, bf16[128,1024]{1,0:T(8,128)(2,1)}, u32[]{:S(2)}, u32[]{:S(2)}) collective-permute-start(bf16[128,1024]{1,0:T(8,128)(2,1)S(1)} %pad_maximum_fusion.4.refs_8_.refs_18_), channel_id=1, source_target_pairs={{0,8},{1,9},{2,10},{3,11},{4,12},{5,13},{6,14},{7,15},{8,16},{9,17... | collective-permute-start | bytes 786440 | tf_op jit(solution)/shard_map/ppermute | solution.py:69
  8.0 6.3 %collective-permute-start.3 = (bf16[128,1024]{1,0:T(8,128)(2,1)S(1)}, bf16[128,1024]{1,0:T(8,128)(2,1)}, u32[]{:S(2)}, u32[]{:S(2)}) collective-permute-start(bf16[128,1024]{1,0:T(8,128)(2,1)S(1)} %pad_maximum_fusion.4.refs_8_.refs_18_), channel_id=1, source_target_pairs={{0,6},{1,7},{2,8},{3,9},{4,10},{5,11},{6,12},{7,13},{8,14},{9,15},... | collective-permute-start | bytes 786440 | tf_op jit(solution)/shard_map/ppermute | solution.py:69
  16.5 5.7 %collective-permute-start.2 = (bf16[128,1024]{1,0:T(8,128)(2,1)}, bf16[128,1024]{1,0:T(8,128)(2,1)}, u32[]{:S(2)}, u32[]{:S(2)}) collective-permute-start(bf16[128,1024]{1,0:T(8,128)(2,1)} %pad_maximum_fusion.5), channel_id=1, source_target_pairs={{0,9},{1,8},{2,11},{3,10},{4,13},{5,12},{6,15},{7,14},{8,17},{9,16... | collective-permute-start | bytes 786440 | tf_op jit(solution)/shard_map/ppermute | solution.py:69
  27.7 11.1 %collective-permute-start.19 = (bf16[2,64,2048]{2,1,0:T(8,128)(2,1)}, bf16[2,64,2048]{2,1,0:T(8,128)(2,1)S(1)}, u32[]{:S(2)}, u32[]{:S(2)}) collective-permute-start(bf16[2,64,2048]{2,1,0:T(8,128)(2,1)} %maximum_select_fusion.3), channel_id=1, source_target_pairs={{0,64},{1,65},{2,66},{3,67},{4,68},{5,69},{6,70},{7,71},{8,72},{9,... | collective-permute-start | bytes 1572872 | tf_op jit(solution)/shard_map/ppermute | solution.py:36
  48.1 5.0 %collective-permute-start.7 = (bf16[128,1024]{1,0:T(8,128)(2,1)S(1)}, bf16[128,1024]{1,0:T(8,128)(2,1)S(1)}, u32[]{:S(2)}, u32[]{:S(2)}) collective-permute-start(bf16[128,1024]{1,0:T(8,128)(2,1)S(1)} %pad_maximum_fusion.4.refs_8_.refs_18_), channel_id=1, source_target_pairs={{0,2},{1,3},{2,4},{3,5},{4,6},{5,7},{6,8},{7,9},{8,10},{9,11},{10,... | collective-permute-start | bytes 786440 | tf_op jit(solution)/shard_map/ppermute | solution.py:69
  59.7 12.8 %collective-permute-done.6.refs_5_.refs_15_ = bf16[128,1024]{1,0:T(8,128)(2,1)} collective-permute-done((bf16[128,1024]{1,0:T(8,128)(2,1)}, bf16[128,1024]{1,0:T(8,128)(2,1)}, u32[]{:S(2)}, u32[]{:S(2)}) %collective-permute-start.6) | collective-permute-done | bytes 262176 | tf_op jit(solution)/shard_map/ppermute | solution.py:69
  74.6 12.8 %attend.1 = bf16[2,2,256,512]{3,2,1,0:T(8,128)(2,1)} custom-call(s32[1]{0:T(128)} %bitcast.core_ref, s32[2,9]{1,0:T(2,128)} %copy.27.seen_ref, bf16[256,2048]{1,0:T(8,128)(2,1)} %maximum_select_fusion.1.query_ref, bf16[128,1024]{1,0:T(8,128)(2,1)} %collective-permute-done.1.refs_0_.refs_10_, bf16[128,1024]{1,0:T(8,128)(2,1)} %collective-permute-done.2.refs_1_.refs_11_, ...), custom_call_target="tpu_custom_call" | custom-call | flops 6000000000 | bytes 6000000 | tf_op jit(solution)/shard_map/attend/pallas_call | solution.py:135
  88.6 6.1 %collective-permute-start.14 = (bf16[256,512]{1,0:T(8,128)(2,1)S(1)}, bf16[256,512]{1,0:T(8,128)(2,1)S(1)}, u32[]{:S(2)}, u32[]{:S(2)}) collective-permute-start(bf16[256,512]{1,0:T(8,128)(2,1)S(1)} %get-tuple-element.71), channel_id=1, source_target_pairs={{0,97},{1,32},{2,99},{3,34},{4,101},{5,36},{6,103},{7,38},{8,105},... | collective-permute-start | bytes 786440 | tf_op jit(solution)/shard_map/ppermute | solution.py:36
  94.7 4.2 %collective-permute-start.11 = (bf16[256,512]{1,0:T(8,128)(2,1)S(1)}, bf16[256,512]{1,0:T(8,128)(2,1)S(1)}, u32[]{:S(2)}, u32[]{:S(2)}) collective-permute-start(bf16[256,512]{1,0:T(8,128)(2,1)S(1)} %get-tuple-element.71), channel_id=1, source_target_pairs={{0,32},{1,97},{2,34},{3,99},{4,36},{5,101},{6,38},{7,103},{8,40},{... | collective-permute-start | bytes 786440 | tf_op jit(solution)/shard_map/ppermute | solution.py:36
  109.7 8.7 %collective-permute-done.22 = bf16[2,2,64,1024]{3,2,1,0:T(8,128)(2,1)S(1)} collective-permute-done((bf16[2,2,64,1024]{3,2,1,0:T(8,128)(2,1)S(1)}, bf16[2,2,64,1024]{3,2,1,0:T(8,128)(2,1)S(1)}, u32[]{:S(2)}, u32[]{:S(2)}) %collective-permute-start.22) | collective-permute-done | bytes 524320 | tf_op jit(solution)/shard_map/ppermute | solution.py:36
  120.3 4.8 %collective-permute-done.13 = bf16[256,512]{1,0:T(8,128)(2,1)S(1)} collective-permute-done((bf16[256,512]{1,0:T(8,128)(2,1)S(1)}, bf16[256,512]{1,0:T(8,128)(2,1)S(1)}, u32[]{:S(2)}, u32[]{:S(2)}) %collective-permute-start.13) | collective-permute-done | bytes 262176 | tf_op jit(solution)/shard_map/ppermute | solution.py:36
  125.9 8.2 %project.1 = (bf16[128,2048]{1,0:T(8,128)(2,1)}, bf16[128,2048]{1,0:T(8,128)(2,1)}, bf16[128,2048]{1,0:T(8,128)(2,1)}, bf16[128,2048]{1,0:T(8,128)(2,1)}, bf16[1...) custom-call(s32[1]{0:T(128)} %bitcast.core_ref, ...), custom_call_target="tpu_custom_call" | custom-call | flops 4300000256 | bytes 10000000 | tf_op jit(solution)/shard_map/project/pallas_call | solution.py:195
  139.7 6.9 %collective-permute-done.27 = bf16[128,2048]{1,0:T(8,128)(2,1)S(1)} collective-permute-done((bf16[128,2048]{1,0:T(8,128)(2,1)}, bf16[128,2048]{1,0:T(8,128)(2,1)S(1)}, u32[]{:S(2)}, u32[]{:S(2)}) %collective-permute-start.27) | collective-permute-done | bytes 524320 | tf_op jit(solution)/shard_map/ppermute | solution.py:36
  152.5 5.4 %collective-permute-done.24 = bf16[128,2048]{1,0:T(8,128)(2,1)S(1)} collective-permute-done((bf16[128,2048]{1,0:T(8,128)(2,1)}, bf16[128,2048]{1,0:T(8,128)(2,1)S(1)}, u32[]{:S(2)}, u32[]{:S(2)}) %collective-permute-start.24) | collective-permute-done | bytes 524320 | tf_op jit(solution)/shard_map/ppermute | solution.py:36
  158.3 5.1 %collective-permute-done.26 = bf16[128,2048]{1,0:T(8,128)(2,1)S(1)} collective-permute-done((bf16[128,2048]{1,0:T(8,128)(2,1)}, bf16[128,2048]{1,0:T(8,128)(2,1)S(1)}, u32[]{:S(2)}, u32[]{:S(2)}) %collective-permute-start.26) | collective-permute-done | bytes 524320 | tf_op jit(solution)/shard_map/ppermute | solution.py:36
  172.4 5.0 %collective-permute-done.31 = bf16[40,4096]{1,0:T(8,128)(2,1)S(1)} collective-permute-done((bf16[40,4096]{1,0:T(8,128)(2,1)S(1)}, bf16[40,4096]{1,0:T(8,128)(2,1)S(1)}, u32[]{:S(2)}, u32[]{:S(2)}) %collective-permute-start.31) | collective-permute-done | bytes 327712 | tf_op jit(solution)/shard_map/ppermute | solution.py:36
  190.7 6.8 %collective-permute-done.34 = bf16[80,4096]{1,0:T(8,128)(2,1)S(1)} collective-permute-done((bf16[80,4096]{1,0:T(8,128)(2,1)S(1)}, bf16[80,4096]{1,0:T(8,128)(2,1)S(1)}, u32[]{:S(2)}, u32[]{:S(2)}) %collective-permute-start.34) | collective-permute-done | bytes 655392 | tf_op jit(solution)/shard_map/ppermute | solution.py:36
  199.1 12.3 %collective-permute-done.47 = bf16[80,4096]{1,0:T(8,128)(2,1)S(1)} collective-permute-done((bf16[80,4096]{1,0:T(8,128)(2,1)S(1)}, bf16[80,4096]{1,0:T(8,128)(2,1)S(1)}, u32[]{:S(2)}, u32[]{:S(2)}) %collective-permute-start.47) | collective-permute-done | bytes 655392 | tf_op jit(solution)/shard_map/ppermute | solution.py:36
  214.3 15.5 %expert.2 = (bf16[320,4096]{1,0:T(8,128)(2,1)}, bf16[320,4096]{1,0:T(8,128)(2,1)}) custom-call(bf16[160,4096]{1,0:T(8,128)(2,1)} %copy-done.2, bf16[160,4096]{1,0:T(8,128)(2,1)} %copy-done.8, bf16[160,4096]{1,0:T(8,128)(2,1)} %copy-done.11, bf16[160,4096]{1,0:T(8,128)(2,1)} %collective-permute-done.37.refs_3_, bf16[2,448,4096]{2,1,0:T(8,128)(2,1)} %refs_4_.3, ...), custom_call_target="tpu_custom_call" | custom-call | flops 7000000000 | bytes 22000000 | tf_op jit(solution)/shard_map/expert/pallas_call | solution.py:262
  230.6 15.6 %expert.3 = (bf16[320,4096]{1,0:T(8,128)(2,1)}, bf16[320,4096]{1,0:T(8,128)(2,1)}) custom-call(bf16[160,4096]{1,0:T(8,128)(2,1)} %copy-done.3, bf16[160,4096]{1,0:T(8,128)(2,1)} %constant_dynamic-update-slice_fusion.2.refs_1_, bf16[160,4096]{1,0:T(8,128)(2,1)} %collective-permute-done.49.refs_2_, bf16[160,4096]{1,0:T(8,128)(2,1)} %collective-permute-done.50.refs_3_, ...), custom_call_target="tpu_custom_call" | custom-call | flops 7000000000 | bytes 22000000 | tf_op jit(solution)/shard_map/expert/pallas_call | solution.py:262
  258.7 4.9 %collective-permute-done.42 = bf16[40,4096]{1,0:T(8,128)(2,1)S(1)} collective-permute-done((bf16[40,4096]{1,0:T(8,128)(2,1)S(1)}, bf16[40,4096]{1,0:T(8,128)(2,1)S(1)}, u32[]{:S(2)}, u32[]{:S(2)}) %collective-permute-start.42) | collective-permute-done | bytes 327712 | tf_op jit(solution)/shard_map/ppermute | solution.py:36
  266.8 6.9 %collective-permute-done.55 = bf16[40,4096]{1,0:T(8,128)(2,1)S(1)} collective-permute-done((bf16[40,4096]{1,0:T(8,128)(2,1)S(1)}, bf16[40,4096]{1,0:T(8,128)(2,1)S(1)}, u32[]{:S(2)}, u32[]{:S(2)}) %collective-permute-start.55) | collective-permute-done | bytes 327712 | tf_op jit(solution)/shard_map/ppermute | solution.py:36
  282.2 15.0 %collective-permute-done.53 = bf16[80,4096]{1,0:T(8,128)(2,1)S(1)} collective-permute-done((bf16[80,4096]{1,0:T(8,128)(2,1)S(1)}, bf16[80,4096]{1,0:T(8,128)(2,1)S(1)}, u32[]{:S(2)}, u32[]{:S(2)}) %collective-permute-start.53) | collective-permute-done | bytes 655392 | tf_op jit(solution)/shard_map/ppermute | solution.py:36
  300.9 7.0 %collective-permute-done.54 = bf16[40,4096]{1,0:T(8,128)(2,1)S(1)} collective-permute-done((bf16[40,4096]{1,0:T(8,128)(2,1)S(1)}, bf16[40,4096]{1,0:T(8,128)(2,1)S(1)}, u32[]{:S(2)}, u32[]{:S(2)}) %collective-permute-start.54) | collective-permute-done | bytes 327712 | tf_op jit(solution)/shard_map/ppermute | solution.py:36
  (223 shorter events, 111.3 us)
Async XLA Ops:
  1.3 41.1 %collective-permute-start.1 = (bf16[128,1024]{1,0:T(8,128)(2,1)S(1)}, bf16[128,1024]{1,0:T(8,128)(2,1)}, u32[]{:S(2)}, u32[]{:S(2)}) collective-permute-start(bf16[128,1024]{1,0:T(8,128)(2,1)S(1)} %pad_maximum_fusion.4.refs_8_.refs_18_), channel_id=1, source_target_pairs={{0,8},{1,9},{2,10},{3,11},{4,12},{5,13},{6,14},{7,15},{8,16},{9,17... | collective-permute-start | bytes 786440 | tf_op jit(solution)/shard_map/ppermute | solution.py:69
  8.0 40.1 %collective-permute-start.3 = (bf16[128,1024]{1,0:T(8,128)(2,1)S(1)}, bf16[128,1024]{1,0:T(8,128)(2,1)}, u32[]{:S(2)}, u32[]{:S(2)}) collective-permute-start(bf16[128,1024]{1,0:T(8,128)(2,1)S(1)} %pad_maximum_fusion.4.refs_8_.refs_18_), channel_id=1, source_target_pairs={{0,6},{1,7},{2,8},{3,9},{4,10},{5,11},{6,12},{7,13},{8,14},{9,15},... | collective-permute-start | bytes 786440 | tf_op jit(solution)/shard_map/ppermute | solution.py:69
  15.7 23.9 %collective-permute-start = (bf16[128,2048]{1,0:T(8,128)(2,1)}, bf16[128,2048]{1,0:T(8,128)(2,1)S(1)}, u32[]{:S(2)}, u32[]{:S(2)}) collective-permute-start(bf16[128,2048]{1,0:T(8,128)(2,1)} %get-tuple-element.74), channel_id=1, source_target_pairs={{0,1},{1,0},{2,3},{3,2},{4,5},{5,4},{6,7},{7,6},{8,9},{9,8},{10,11... | collective-permute-start | bytes 1572872 | tf_op jit(solution)/shard_map/ppermute | solution.py:36
  16.5 29.4 %collective-permute-start.2 = (bf16[128,1024]{1,0:T(8,128)(2,1)}, bf16[128,1024]{1,0:T(8,128)(2,1)}, u32[]{:S(2)}, u32[]{:S(2)}) collective-permute-start(bf16[128,1024]{1,0:T(8,128)(2,1)} %pad_maximum_fusion.5), channel_id=1, source_target_pairs={{0,9},{1,8},{2,11},{3,10},{4,13},{5,12},{6,15},{7,14},{8,17},{9,16... | collective-permute-start | bytes 786440 | tf_op jit(solution)/shard_map/ppermute | solution.py:69
  27.7 29.7 %collective-permute-start.19 = (bf16[2,64,2048]{2,1,0:T(8,128)(2,1)}, bf16[2,64,2048]{2,1,0:T(8,128)(2,1)S(1)}, u32[]{:S(2)}, u32[]{:S(2)}) collective-permute-start(bf16[2,64,2048]{2,1,0:T(8,128)(2,1)} %maximum_select_fusion.3), channel_id=1, source_target_pairs={{0,64},{1,65},{2,66},{3,67},{4,68},{5,69},{6,70},{7,71},{8,72},{9,... | collective-permute-start | bytes 1572872 | tf_op jit(solution)/shard_map/ppermute | solution.py:36
  45.9 26.6 %collective-permute-start.6 = (bf16[128,1024]{1,0:T(8,128)(2,1)}, bf16[128,1024]{1,0:T(8,128)(2,1)}, u32[]{:S(2)}, u32[]{:S(2)}) collective-permute-start(bf16[128,1024]{1,0:T(8,128)(2,1)} %pad_maximum_fusion.5), channel_id=1, source_target_pairs={{0,5},{1,4},{2,7},{3,6},{4,9},{5,8},{6,11},{7,10},{8,13},{9,12},{1... | collective-permute-start | bytes 786440 | tf_op jit(solution)/shard_map/ppermute | solution.py:69
  48.1 24.4 %collective-permute-start.7 = (bf16[128,1024]{1,0:T(8,128)(2,1)S(1)}, bf16[128,1024]{1,0:T(8,128)(2,1)S(1)}, u32[]{:S(2)}, u32[]{:S(2)}) collective-permute-start(bf16[128,1024]{1,0:T(8,128)(2,1)S(1)} %pad_maximum_fusion.4.refs_8_.refs_18_), channel_id=1, source_target_pairs={{0,2},{1,3},{2,4},{3,5},{4,6},{5,7},{6,8},{7,9},{8,10},{9,11},{10,... | collective-permute-start | bytes 786440 | tf_op jit(solution)/shard_map/ppermute | solution.py:69
  58.2 44.4 %collective-permute-start.20 = (bf16[2,2,64,2048]{3,2,1,0:T(8,128)(2,1)S(1)}, bf16[2,2,64,2048]{3,2,1,0:T(8,128)(2,1)S(1)}, u32[]{:S(2)}, u32[]{:S(2)}) collective-permute-start(bf16[2,2,64,2048]{3,2,1,0:T(8,128)(2,1)S(1)} %bitcast_dynamic-update-slice_fusion.5), channel_id=1, source_target_pairs={{0,16},{1,17},{2,18},{3,19},{4,20},{5,21},{6,22},{7,23},{8,24},{9,... | collective-permute-start | bytes 3145736 | tf_op jit(solution)/shard_map/ppermute | solution.py:36
  72.5 30.2 %collective-permute-start.21 = (bf16[2,2,64,2048]{3,2,1,0:T(8,128)(2,1)S(1)}, bf16[2,2,64,2048]{3,2,1,0:T(8,128)(2,1)S(1)}, u32[]{:S(2)}, u32[]{:S(2)}) collective-permute-start(bf16[2,2,64,2048]{3,2,1,0:T(8,128)(2,1)S(1)} %bitcast_dynamic-update-slice_fusion.5), channel_id=1, source_target_pairs={{0,18},{1,19},{2,16},{3,17},{4,22},{5,23},{6,20},{7,21},{8,26},{9,... | collective-permute-start | bytes 3145736 | tf_op jit(solution)/shard_map/ppermute | solution.py:36
  88.6 19.6 %collective-permute-start.14 = (bf16[256,512]{1,0:T(8,128)(2,1)S(1)}, bf16[256,512]{1,0:T(8,128)(2,1)S(1)}, u32[]{:S(2)}, u32[]{:S(2)}) collective-permute-start(bf16[256,512]{1,0:T(8,128)(2,1)S(1)} %get-tuple-element.71), channel_id=1, source_target_pairs={{0,97},{1,32},{2,99},{3,34},{4,101},{5,36},{6,103},{7,38},{8,105},... | collective-permute-start | bytes 786440 | tf_op jit(solution)/shard_map/ppermute | solution.py:36
  94.7 25.5 %collective-permute-start.11 = (bf16[256,512]{1,0:T(8,128)(2,1)S(1)}, bf16[256,512]{1,0:T(8,128)(2,1)S(1)}, u32[]{:S(2)}, u32[]{:S(2)}) collective-permute-start(bf16[256,512]{1,0:T(8,128)(2,1)S(1)} %get-tuple-element.71), channel_id=1, source_target_pairs={{0,32},{1,97},{2,34},{3,99},{4,36},{5,101},{6,38},{7,103},{8,40},{... | collective-permute-start | bytes 786440 | tf_op jit(solution)/shard_map/ppermute | solution.py:36
  137.3 20.6 %collective-permute-start.24 = (bf16[128,2048]{1,0:T(8,128)(2,1)}, bf16[128,2048]{1,0:T(8,128)(2,1)S(1)}, u32[]{:S(2)}, u32[]{:S(2)}) collective-permute-start(bf16[128,2048]{1,0:T(8,128)(2,1)} %get-tuple-element.29), channel_id=1, source_target_pairs={{0,36},{1,109},{2,38},{3,111},{4,32},{5,105},{6,34},{7,107},{8,44}... | collective-permute-start | bytes 1572872 | tf_op jit(solution)/shard_map/ppermute | solution.py:36
  177.4 20.0 %collective-permute-start.34 = (bf16[80,4096]{1,0:T(8,128)(2,1)S(1)}, bf16[80,4096]{1,0:T(8,128)(2,1)S(1)}, u32[]{:S(2)}, u32[]{:S(2)}) collective-permute-start(bf16[80,4096]{1,0:T(8,128)(2,1)S(1)} %pad_maximum_fusion.2), channel_id=1, source_target_pairs={{0,4},{1,5},{2,6},{3,7},{4,8},{5,9},{6,10},{7,11},{8,12},{9,13},{1... | collective-permute-start | bytes 1966088 | tf_op jit(solution)/shard_map/ppermute | solution.py:36
  178.0 19.5 %collective-permute-start.35 = (bf16[80,4096]{1,0:T(8,128)(2,1)S(1)}, bf16[80,4096]{1,0:T(8,128)(2,1)S(1)}, u32[]{:S(2)}, u32[]{:S(2)}) collective-permute-start(bf16[80,4096]{1,0:T(8,128)(2,1)S(1)} %pad_maximum_fusion.2), channel_id=1, source_target_pairs={{0,12},{1,13},{2,14},{3,15},{4,0},{5,1},{6,2},{7,3},{8,4},{9,5},{1... | collective-permute-start | bytes 1966088 | tf_op jit(solution)/shard_map/ppermute | solution.py:36
  184.5 27.0 %collective-permute-start.47 = (bf16[80,4096]{1,0:T(8,128)(2,1)S(1)}, bf16[80,4096]{1,0:T(8,128)(2,1)S(1)}, u32[]{:S(2)}, u32[]{:S(2)}) collective-permute-start(bf16[80,4096]{1,0:T(8,128)(2,1)S(1)} %pad_maximum_fusion.3), channel_id=1, source_target_pairs={{0,4},{1,5},{2,6},{3,7},{4,8},{5,9},{6,10},{7,11},{8,12},{9,13},{1... | collective-permute-start | bytes 1966088 | tf_op jit(solution)/shard_map/ppermute | solution.py:36
  184.6 27.8 %collective-permute-start.48 = (bf16[80,4096]{1,0:T(8,128)(2,1)S(1)}, bf16[80,4096]{1,0:T(8,128)(2,1)S(1)}, u32[]{:S(2)}, u32[]{:S(2)}) collective-permute-start(bf16[80,4096]{1,0:T(8,128)(2,1)S(1)} %pad_maximum_fusion.3), channel_id=1, source_target_pairs={{0,12},{1,13},{2,14},{3,15},{4,0},{5,1},{6,2},{7,3},{8,4},{9,5},{1... | collective-permute-start | bytes 1966088 | tf_op jit(solution)/shard_map/ppermute | solution.py:36
  199.0 31.6 %collective-permute-start.49 = (bf16[160,4096]{1,0:T(8,128)(2,1)S(1)}, bf16[160,4096]{1,0:T(8,128)(2,1)}, u32[]{:S(2)}, u32[]{:S(2)}) collective-permute-start(bf16[160,4096]{1,0:T(8,128)(2,1)S(1)} %pad_maximum_fusion.1.refs_0_), channel_id=1, source_target_pairs={{0,1},{1,0},{2,3},{3,2},{4,5},{5,4},{6,7},{7,6},{8,9},{9,8},{10,11... | collective-permute-start | bytes 3932168 | tf_op jit(solution)/shard_map/ppermute | solution.py:36
  250.5 23.8 %collective-permute-start.39 = (bf16[80,4096]{1,0:T(8,128)(2,1)S(1)}, bf16[80,4096]{1,0:T(8,128)(2,1)S(1)}, u32[]{:S(2)}, u32[]{:S(2)}) collective-permute-start(bf16[80,4096]{1,0:T(8,128)(2,1)S(1)} %get-tuple-element.40), channel_id=1, source_target_pairs={{0,12},{1,13},{2,14},{3,15},{4,0},{5,1},{6,2},{7,3},{8,4},{9,5},{1... | collective-permute-start | bytes 1966088 | tf_op jit(solution)/shard_map/ppermute | solution.py:36
  251.2 26.2 %collective-permute-start.40 = (bf16[80,4096]{1,0:T(8,128)(2,1)S(1)}, bf16[80,4096]{1,0:T(8,128)(2,1)S(1)}, u32[]{:S(2)}, u32[]{:S(2)}) collective-permute-start(bf16[80,4096]{1,0:T(8,128)(2,1)S(1)} %get-tuple-element.41), channel_id=1, source_target_pairs={{0,4},{1,5},{2,6},{3,7},{4,8},{5,9},{6,10},{7,11},{8,12},{9,13},{1... | collective-permute-start | bytes 1966088 | tf_op jit(solution)/shard_map/ppermute | solution.py:36
  256.6 25.7 %collective-permute-start.52 = (bf16[80,4096]{1,0:T(8,128)(2,1)S(1)}, bf16[80,4096]{1,0:T(8,128)(2,1)S(1)}, u32[]{:S(2)}, u32[]{:S(2)}) collective-permute-start(bf16[80,4096]{1,0:T(8,128)(2,1)S(1)} %get-tuple-element.48), channel_id=1, source_target_pairs={{0,12},{1,13},{2,14},{3,15},{4,0},{5,1},{6,2},{7,3},{8,4},{9,5},{1... | collective-permute-start | bytes 1966088 | tf_op jit(solution)/shard_map/ppermute | solution.py:36
  258.4 38.8 %collective-permute-start.53 = (bf16[80,4096]{1,0:T(8,128)(2,1)S(1)}, bf16[80,4096]{1,0:T(8,128)(2,1)S(1)}, u32[]{:S(2)}, u32[]{:S(2)}) collective-permute-start(bf16[80,4096]{1,0:T(8,128)(2,1)S(1)} %get-tuple-element.49), channel_id=1, source_target_pairs={{0,4},{1,5},{2,6},{3,7},{4,8},{5,9},{6,10},{7,11},{8,12},{9,13},{1... | collective-permute-start | bytes 1966088 | tf_op jit(solution)/shard_map/ppermute | solution.py:36
  273.7 27.0 %collective-permute-start.43 = (bf16[40,4096]{1,0:T(8,128)(2,1)S(1)}, bf16[40,4096]{1,0:T(8,128)(2,1)S(1)}, u32[]{:S(2)}, u32[]{:S(2)}) collective-permute-start(bf16[40,4096]{1,0:T(8,128)(2,1)S(1)} %add_convert_fusion.10), channel_id=1, source_target_pairs={{0,8},{1,9},{2,10},{3,11},{4,12},{5,13},{6,14},{7,15},{8,0},{9,1},... | collective-permute-start | bytes 983048 | tf_op jit(solution)/shard_map/ppermute | solution.py:36
  274.3 26.6 %collective-permute-start.56 = (bf16[40,4096]{1,0:T(8,128)(2,1)S(1)}, bf16[40,4096]{1,0:T(8,128)(2,1)S(1)}, u32[]{:S(2)}, u32[]{:S(2)}) collective-permute-start(bf16[40,4096]{1,0:T(8,128)(2,1)S(1)} %add_convert_fusion.4), channel_id=1, source_target_pairs={{0,8},{1,9},{2,10},{3,11},{4,12},{5,13},{6,14},{7,15},{8,0},{9,1},... | collective-permute-start | bytes 983048 | tf_op jit(solution)/shard_map/ppermute | solution.py:36
  277.5 23.2 %collective-permute-start.41 = (bf16[40,4096]{1,0:T(8,128)(2,1)S(1)}, bf16[40,4096]{1,0:T(8,128)(2,1)S(1)}, u32[]{:S(2)}, u32[]{:S(2)}) collective-permute-start(bf16[40,4096]{1,0:T(8,128)(2,1)S(1)} %add_convert_fusion.11), channel_id=1, source_target_pairs={{0,2},{1,3},{2,0},{3,1},{4,6},{5,7},{6,4},{7,5},{8,10},{9,11},{10,... | collective-permute-start | bytes 983048 | tf_op jit(solution)/shard_map/ppermute | solution.py:36
  (66 other events, 840.8 us)
